TPU v7x, 32 devices: a whole 2x2x4 slice. The times are simulated.
32 devices in a mesh: gx: 4 (over x, core), gy: 4 (over z), gz: 2 (over y).
Axes of the slice: x: 2, y: 2, z: 4, core: 2. Of those that a mesh axis runs over, the one named last changes fastest.
Arguments:
- embeds: bfloat16 [256, 128, 2048], P(('gx', 'gy', 'gz')), may hold values from -6 to 6
- dest_device: int32 [256], P(('gx', 'gy', 'gz')), may hold values from 0 to 31, as said below
- shuffle_key: int32 [256], P(('gx', 'gy', 'gz')), may hold values from 0 to 255, each once
- lengths: int32 [8], replicated, may hold values from 1 to 4096
- gain: float32 [2048], replicated, may hold values from 0.1 to 1.9
Outputs:
- packed: bfloat16 [512, 128, 2048], P(('gx', 'gy', 'gz'))
Inputs may be any that keep to these rules, and one draw needn't show every extreme that they name: `dest_device`: device numbers are ((gx * 4) + gy) * 2 + gz. A device receives at most 16 tiles, and in every draw some devices receive exactly 16. The 2 devices sharing gx and gy send at most one tile to any one device and exactly 8 tiles to the devices of each gz index. Of one device's tiles at most 4 go to devices of one gz index, and some device reaches that.
All inputs are finite; a program needn't handle non-finite values.
Results may differ from a plain program's by a relative error of at most 0.001.
Values may be sent and summed in bfloat16 or wider, within the bound.
A program may use at most 128 MiB of HBM per device.

v0:
```python
import functools

import jax
import jax.numpy as jnp
from jax import lax
from jax.experimental import pallas as pl
from jax.experimental.pallas import tpu as pltpu
from jax.sharding import PartitionSpec as P

TILES_SEQ = 32
CLASSES = (9, 10, 11, 12, 13, 16)
CHUNKS = (2,) * 32
LATENCY = 11
AHEAD = 1
MESH = pl.DeviceIdType.MESH


def exchange_kernel(
    sizes, small_in, x_ref, gain_ref, recv_ref, keys_ref,
    small_ref, gain, small_sem, first_table, limit_table, note_out, notes, note_table, second, keys_out,
    x_sem, gain_sem, y_send, y_recv, g_send, g_recv, own_sem,
    note_send, note_recv, note_sem, key_send, key_recv, *buffers,
):
    nx, ny, depth, per_peer, chunk_rows = sizes
    chunks = len(chunk_rows)
    starts = [sum(chunk_rows[:c]) for c in range(chunks)]
    groups = nx * ny
    tiles_here, tile_rows, _ = x_ref.shape
    raw, first, arrived, outgoing = (buffers[i * chunks : (i + 1) * chunks] for i in range(4))
    gx, gy, gz = lax.axis_index("gx"), lax.axis_index("gy"), lax.axis_index("gz")
    group = gx * ny + gy
    me = group * depth + gz
    offsets = [(dx, dy) for dy in sorted(range(ny), key=lambda d: abs(d - ny // 2)) for dx in range(nx)]
    offsets.remove((0, 0))

    def load(c):
        return pltpu.make_async_copy(
            x_ref.at[:, pl.ds(starts[c], chunk_rows[c])], raw[c], x_sem.at[c]
        )

    def fill_tables():
        depths = [lax.rem(small_ref[0, i], depth) for i in range(tiles_here)]
        dest_groups = [lax.div(small_ref[0, i], depth) for i in range(tiles_here)]
        places, limits = [], []
        for i in range(tiles_here):
            spot = jnp.int32(0)
            for j in range(i):
                spot = spot + jnp.where(depths[j] == depths[i], 1, 0)
            places.append(depths[i] * per_peer + spot)
            tile = me * tiles_here + i
            length = small_ref[0, 2 * tiles_here + tile // TILES_SEQ]
            limits.append(jnp.maximum(length - tile % TILES_SEQ * tile_rows, 0))
        lane = lax.broadcasted_iota(jnp.int32, note_out.shape[1:], 1)
        for z in range(depth):
            row = jnp.zeros(note_out.shape[1:], jnp.int32)
            for p in range(per_peer):
                slot = z * per_peer + p
                tile, limit, dest_group, key = (jnp.int32(v) for v in (0, 0, -1, 0))
                for i in range(tiles_here):
                    hit = places[i] == slot
                    tile = jnp.where(hit, i, tile)
                    limit = jnp.where(hit, limits[i], limit)
                    dest_group = jnp.where(hit, dest_groups[i], dest_group)
                    key = jnp.where(hit, small_ref[0, tiles_here + i] + 1, key)
                first_table[slot] = tile
                limit_table[slot] = limit
                row = jnp.where(lane == p, dest_group, row)
                row = jnp.where(lane == per_peer + p, key, row)
            note_out[z] = row

    def normed(c, slot):
        rows = chunk_rows[c]
        values = raw[c][first_table[slot]].astype(jnp.float32)
        meansq = jnp.mean(values * values, axis=-1, keepdims=True)
        scaled = values * lax.rsqrt(jnp.maximum(meansq, 0.25)) * gain[...]
        row = starts[c] + lax.broadcasted_iota(jnp.int32, (rows, 1), 0)
        return jnp.where(row < limit_table[slot], scaled, 0.0).astype(jnp.bfloat16)

    def y_copy(c, dz, peer, origin):
        return pltpu.make_async_remote_copy(
            src_ref=first[c].at[dz - 1],
            dst_ref=arrived[c].at[pl.ds(origin * per_peer, per_peer)],
            send_sem=y_send.at[c, dz - 1],
            recv_sem=y_recv.at[c, dz - 1],
            device_id=(gx, gy, peer),
            device_id_type=MESH,
        )

    def peer_of(k):
        dx, dy = offsets[k]
        return lax.rem(gx + dx, nx), lax.rem(gy + dy, ny)

    def g_copy(c, k, px, py, origin):
        return pltpu.make_async_remote_copy(
            src_ref=outgoing[c].at[k],
            dst_ref=recv_ref.at[origin, pl.ds(starts[c], chunk_rows[c])],
            send_sem=g_send.at[c, k],
            recv_sem=g_recv.at[c, k],
            device_id=(px, py, gz),
            device_id_type=MESH,
        )

    def own_copy(c):
        return pltpu.make_async_copy(
            outgoing[c].at[groups - 1],
            recv_ref.at[group, pl.ds(starts[c], chunk_rows[c])],
            own_sem.at[c],
        )

    def note_copy(dz, peer, place):
        return pltpu.make_async_remote_copy(
            src_ref=note_out.at[peer],
            dst_ref=notes.at[place],
            send_sem=note_send.at[dz - 1],
            recv_sem=note_recv.at[dz - 1],
            device_id=(gx, gy, peer),
            device_id_type=MESH,
        )

    def key_copy(k, px, py, place):
        return pltpu.make_async_remote_copy(
            src_ref=keys_out.at[k],
            dst_ref=keys_ref.at[place],
            send_sem=key_send.at[k],
            recv_sem=key_recv.at[k],
            device_id=(px, py, gz),
            device_id_type=MESH,
        )

    def prepare(c):
        load(c).wait()
        for dz in range(1, depth):
            peer = lax.rem(gz + dz, depth)
            for p in range(per_peer):
                first[c][dz - 1, p] = normed(c, peer * per_peer + p)
        for p in range(per_peer):
            arrived[c][gz * per_peer + p] = normed(c, gz * per_peer + p)

    def send_first(c):
        for dz in range(1, depth):
            y_copy(c, dz, lax.rem(gz + dz, depth), gz).start()

    def find_slots():
        for dz in range(1, depth):
            origin = lax.rem(gz + depth - dz, depth)
            note_copy(dz, origin, origin).wait()
        tables = [
            pltpu.make_async_copy(
                notes.at[lax.rem(gz + dz, depth)], note_table.at[lax.rem(gz + dz, depth)], note_sem.at[dz]
            )
            for dz in range(1, depth)
        ]
        tables.append(pltpu.make_async_copy(note_out.at[gz], note_table.at[gz], note_sem.at[0]))
        for copy in tables:
            copy.start()
        for copy in tables:
            copy.wait()

        for k in range(groups):
            px, py = peer_of(k) if k < groups - 1 else (gx, gy)
            wanted = px * ny + py
            slot, key = jnp.int32(0), jnp.int32(0)
            for z in range(depth):
                for p in range(per_peer):
                    hit = note_table[z, 0, p] == wanted
                    slot = jnp.where(hit, z * per_peer + p, slot)
                    key = jnp.where(hit, note_table[z, 0, per_peer + p], key)
            second[k] = slot
            row = jnp.full(keys_out.shape[1:], key, jnp.int32)
            if k < groups - 1:
                keys_out[k] = row
            else:
                keys_ref[group] = row

    def forward(c):
        for dz in range(1, depth):
            origin = lax.rem(gz + depth - dz, depth)
            y_copy(c, dz, origin, origin).wait_recv()
        for k in range(groups):
            outgoing[c][k] = arrived[c][second[k]]
        for k in range(groups - 1):
            px, py = peer_of(k)
            g_copy(c, k, px, py, group).start()
        own_copy(c).start()

    small = [
        pltpu.make_async_copy(small_in, small_ref, small_sem),
        pltpu.make_async_copy(gain_ref, gain, gain_sem),
    ]
    for copy in small:
        copy.start()
    for c in range(chunks):
        load(c).start()
    barrier = pltpu.get_barrier_semaphore()
    for dz in range(1, depth):
        pl.semaphore_signal(
            barrier, inc=1, device_id=(gx, gy, lax.rem(gz + dz, depth)), device_id_type=MESH
        )
    for k in range(groups - 1):
        px, py = peer_of(k)
        pl.semaphore_signal(barrier, inc=1, device_id=(px, py, gz), device_id_type=MESH)
    for copy in small:
        copy.wait()
    fill_tables()
    prepare(0)
    pl.semaphore_wait(barrier, depth - 1 + groups - 1)
    for dz in range(1, depth):
        note_copy(dz, lax.rem(gz + dz, depth), gz).start()
    send_first(0)
    if chunks > 1:
        prepare(1)
        send_first(1)
    find_slots()
    forward(0)
    for k in range(groups - 1):
        px, py = peer_of(k)
        key_copy(k, px, py, group).start()
    for c in range(2, chunks):
        prepare(c)
        send_first(c)
        forward(c - 1)
    if chunks > 1:
        forward(chunks - 1)

    for c in range(chunks):
        for dz in range(1, depth):
            y_copy(c, dz, lax.rem(gz + dz, depth), gz).wait_send()
    sources = []
    for dx, dy in offsets:
        sources.append((lax.rem(gx + nx - dx, nx), lax.rem(gy + ny - dy, ny)))
    for k, (sx, sy) in enumerate(sources):
        key_copy(k, sx, sy, sx * ny + sy).wait()
    for c in range(chunks):
        for k, (sx, sy) in enumerate(sources):
            g_copy(c, k, sx, sy, sx * ny + sy).wait()
        own_copy(c).wait()


def place_kernel(source_ref, filled_ref, blocks_ref, out_ref, zeros, out_sem):
    cap = out_ref.shape[0]

    def store(slot):
        return pltpu.make_async_copy(blocks_ref.at[source_ref[slot]], out_ref.at[slot], out_sem.at[slot])

    for slot in range(cap):
        pl.when(filled_ref[slot] == 1)(lambda slot=slot: store(slot).start())
    zeros[...] = jnp.zeros_like(zeros)
    for slot in range(cap):

        @pl.when(filled_ref[slot] == 0)
        def _():
            pltpu.make_async_copy(zeros, out_ref.at[slot], out_sem.at[slot]).start()

    for slot in range(cap):
        store(slot).wait()


def direct(embeds, dest_device, shuffle_key, lengths, gain):
    tiles_here, tile_rows, width = embeds.shape
    nx, ny, depth = lax.axis_size("gx"), lax.axis_size("gy"), lax.axis_size("gz")
    groups = nx * ny
    per_peer = (tiles_here + depth - 1) // depth
    slots = depth * per_peer
    chunk_rows = (tile_rows,)
    if tile_rows % 128 == 0:
        chunk_rows = tuple(part * tile_rows // 16 for part in (1, 1, 2, 2, 4, 4, 2))
    chunks = len(chunk_rows)

    smem = pl.BlockSpec(memory_space=pltpu.SMEM)
    vmem = pl.BlockSpec(memory_space=pltpu.VMEM)
    hbm = pl.BlockSpec(memory_space=pl.ANY)
    lanes = -(-2 * per_peer // 128) * 128
    small = jnp.concatenate([dest_device, shuffle_key, lengths])
    small = jnp.pad(small, (0, -small.shape[0] % 128))[None, :]
    received, key_rows = pl.pallas_call(
        functools.partial(exchange_kernel, (nx, ny, depth, per_peer, chunk_rows)),
        out_shape=(
            jax.ShapeDtypeStruct((groups, tile_rows, width), jnp.bfloat16),
            jax.ShapeDtypeStruct((groups, 1, 128), jnp.int32),
        ),
        in_specs=[hbm] * 3,
        out_specs=(hbm, vmem),
        scratch_shapes=[
            pltpu.SMEM(small.shape, jnp.int32),
            pltpu.VMEM((1, width), jnp.float32),
            pltpu.SemaphoreType.DMA,
            pltpu.SMEM((slots,), jnp.int32),
            pltpu.SMEM((slots,), jnp.int32),
            pltpu.VMEM((depth, 1, lanes), jnp.int32),
            pltpu.VMEM((depth, 1, lanes), jnp.int32),
            pltpu.SMEM((depth, 1, lanes), jnp.int32),
            pltpu.SMEM((groups,), jnp.int32),
            pltpu.VMEM((groups, 1, 128), jnp.int32),
            pltpu.SemaphoreType.DMA((chunks,)),
            pltpu.SemaphoreType.DMA,
            pltpu.SemaphoreType.DMA((chunks, depth - 1)),
            pltpu.SemaphoreType.DMA((chunks, depth - 1)),
            pltpu.SemaphoreType.DMA((chunks, groups)),
            pltpu.SemaphoreType.DMA((chunks, groups)),
            pltpu.SemaphoreType.DMA((chunks,)),
            pltpu.SemaphoreType.DMA((depth,)),
            pltpu.SemaphoreType.DMA((depth,)),
            pltpu.SemaphoreType.DMA((depth,)),
            pltpu.SemaphoreType.DMA((groups,)),
            pltpu.SemaphoreType.DMA((groups,)),
        ]
        + [pltpu.VMEM((tiles_here, rows, width), jnp.bfloat16) for rows in chunk_rows]
        + [pltpu.VMEM((depth - 1, per_peer, rows, width), jnp.bfloat16) for rows in chunk_rows]
        + [pltpu.VMEM((slots, rows, width), jnp.bfloat16) for rows in chunk_rows]
        + [pltpu.VMEM((groups, rows, width), jnp.bfloat16) for rows in chunk_rows],
        compiler_params=pltpu.CompilerParams(
            collective_id=0, has_side_effects=True, vmem_limit_bytes=36 * 1024 * 1024
        ),
        name="exchange",
    )(small, embeds, gain.reshape(1, width))

    key_of = key_rows[:, 0, 0]
    valid = key_of > 0
    rank = jnp.sum((valid[None, :] & (key_of[None, :] < key_of[:, None])).astype(jnp.int32), axis=1)
    cap = 2 * tiles_here
    at = valid[None, :] & (rank[None, :] == jnp.arange(cap, dtype=jnp.int32)[:, None])
    source = jnp.sum(jnp.where(at, jnp.arange(groups, dtype=jnp.int32)[None, :], 0), axis=1).astype(jnp.int32)
    filled = jnp.sum(at.astype(jnp.int32), axis=1).astype(jnp.int32)

    return pl.pallas_call(
        place_kernel,
        out_shape=jax.ShapeDtypeStruct((cap, tile_rows, width), jnp.bfloat16),
        in_specs=[smem, smem, vmem],
        out_specs=hbm,
        scratch_shapes=[
            pltpu.VMEM((tile_rows, width), jnp.bfloat16),
            pltpu.SemaphoreType.DMA((cap,)),
        ],
        compiler_params=pltpu.CompilerParams(vmem_limit_bytes=24 * 1024 * 1024),
        name="place",
    )(source, filled, received)


def table_kernel(
    sizes, dest_hbm, key_hbm, lengths_hbm, x_ref, gain_hbm, table_ref, normed_ref,
    dest_ref, lengths_ref, dest_row, key_row, gain_ref, small_sem, mine, first_table, limit_table, raw, done, send, recv, x_sem, out_sem,
):
    nx, ny, depth, per_peer = sizes
    devices = nx * ny * depth
    tiles_here, tile_rows, width = x_ref.shape
    slots = depth * per_peer
    block = 16
    me = (lax.axis_index("gx") * ny + lax.axis_index("gy")) * depth + lax.axis_index("gz")

    def place_of(device):
        return lax.div(device, ny * depth), lax.rem(lax.div(device, depth), ny), lax.rem(device, depth)

    def row_copy(step, target, row):
        return pltpu.make_async_remote_copy(
            src_ref=mine,
            dst_ref=table_ref.at[row],
            send_sem=send.at[step - 1],
            recv_sem=recv.at[step - 1],
            device_id=place_of(target),
            device_id_type=MESH,
        )

    def normalize(slot):
        @pl.loop(0, tile_rows // block, unroll=4)
        def _(part):
            start = part * block
            values = raw[first_table[slot], pl.ds(start, block)].astype(jnp.float32)
            meansq = jnp.mean(values * values, axis=-1, keepdims=True)
            scaled = values * lax.rsqrt(jnp.maximum(meansq, 0.25)) * gain_ref[...]
            row = start + lax.broadcasted_iota(jnp.int32, (block, 1), 0)
            done[slot, pl.ds(start, block)] = jnp.where(row < limit_table[slot], scaled, 0.0).astype(jnp.bfloat16)

        pltpu.make_async_copy(done.at[slot], normed_ref.at[slot], out_sem.at[slot]).start()

    small = [
        pltpu.make_async_copy(dest_hbm, dest_row, small_sem.at[0]),
        pltpu.make_async_copy(key_hbm, key_row, small_sem.at[1]),
        pltpu.make_async_copy(dest_hbm, dest_ref, small_sem.at[2]),
        pltpu.make_async_copy(lengths_hbm, lengths_ref, small_sem.at[3]),
        pltpu.make_async_copy(gain_hbm, gain_ref, small_sem.at[4]),
    ]
    load = pltpu.make_async_copy(x_ref, raw, x_sem)
    for copy in small:
        copy.start()
    load.start()
    barrier = pltpu.get_barrier_semaphore()
    for step in range(1, devices):
        pl.semaphore_signal(
            barrier, inc=1, device_id=place_of(lax.rem(me + step, devices)), device_id_type=MESH
        )
    for copy in small:
        copy.wait()
    mine[...] = jnp.zeros_like(mine)
    mine[0:1, 0:tiles_here] = dest_row[...]
    mine[1:2, 0:tiles_here] = key_row[...]
    table_ref[me] = mine[...]

    pl.semaphore_wait(barrier, devices - 1)
    for step in range(1, devices):
        row_copy(step, lax.rem(me + step, devices), me).start()
    depths = [lax.rem(dest_ref[0, i], depth) for i in range(tiles_here)]
    places, limits = [], []
    for i in range(tiles_here):
        spot = jnp.int32(0)
        for j in range(i):
            spot = spot + jnp.where(depths[j] == depths[i], 1, 0)
        places.append(depths[i] * per_peer + spot)
        tile = me * tiles_here + i
        limits.append(jnp.maximum(lengths_ref[0, tile // TILES_SEQ] - tile % TILES_SEQ * tile_rows, 0))
    for slot in range(slots):
        tile, limit = jnp.int32(0), jnp.int32(0)
        for i in range(tiles_here):
            tile = jnp.where(places[i] == slot, i, tile)
            limit = jnp.where(places[i] == slot, limits[i], limit)
        first_table[slot] = tile
        limit_table[slot] = limit

    load.wait()
    for slot in range(slots):
        normalize(slot)
    for step in range(1, devices):
        source = lax.rem(me + devices - step, devices)
        row_copy(step, source, source).wait()
    for slot in range(slots):
        pltpu.make_async_copy(done.at[slot], normed_ref.at[slot], out_sem.at[slot]).wait()


def line_kernel(
    sizes, plan_ref, x_ref, received,
    plan, plan_sem, x_sem, y_send, y_recv, a_send, a_recv, b_send, b_recv,
    g_send, g_recv, *buffers,
):
    nx, ny, depth, per_peer, pieces, near, far, back, at = sizes
    chunks = len(pieces)
    half = ny // 2
    slots = depth * per_peer
    pool, inflow, inward, outward, outgoing = (
        buffers[i * chunks : (i + 1) * chunks] for i in range(5)
    )
    gx, gy, gz = lax.axis_index("gx"), lax.axis_index("gy"), lax.axis_index("gz")
    low = gy < half
    level = jnp.where(low, gy, ny - 1 - gy)
    inner = jnp.where(low, gy + 1, gy - 1)
    outer = jnp.clip(jnp.where(low, gy - 1, gy + 1), 0, ny - 1)
    middle = level == half - 1

    def piece(ref, start, size, c):
        row, rows, column, columns = pieces[c]
        return ref.at[pl.ds(start, size), pl.ds(row, rows), pl.ds(column, columns)]

    def load(c):
        return pltpu.make_async_copy(
            piece(x_ref, gz * per_peer, per_peer, c),
            pool[c].at[pl.ds(gz * per_peer, per_peer)],
            x_sem.at[c],
        )

    def y_copy(c, dz, peer, origin):
        return pltpu.make_async_remote_copy(
            src_ref=piece(x_ref, peer * per_peer, per_peer, c),
            dst_ref=pool[c].at[pl.ds(origin * per_peer, per_peer)],
            send_sem=y_send.at[c, dz - 1],
            recv_sem=y_recv.at[c, dz - 1],
            device_id=(gx, gy, peer),
            device_id_type=MESH,
        )

    def near_copy(c, peer):
        return pltpu.make_async_remote_copy(
            src_ref=inward[c].at[pl.ds(0, near)],
            dst_ref=pool[c].at[pl.ds(slots, near)],
            send_sem=a_send.at[c],
            recv_sem=a_recv.at[c],
            device_id=(gx, peer, gz),
            device_id_type=MESH,
        )

    def cross_copy(c, peer):
        return pltpu.make_async_remote_copy(
            src_ref=inward[c],
            dst_ref=inflow[c],
            send_sem=a_send.at[c],
            recv_sem=b_recv.at[c],
            device_id=(gx, peer, gz),
            device_id_type=MESH,
        )

    def back_copy(c, peer):
        return pltpu.make_async_remote_copy(
            src_ref=outward[c],
            dst_ref=inflow[c].at[pl.ds(0, back)],
            send_sem=b_send.at[c],
            recv_sem=b_recv.at[c],
            device_id=(gx, peer, gz),
            device_id_type=MESH,
        )

    def g_copy(c, dx, peer, origin):
        return pltpu.make_async_remote_copy(
            src_ref=outgoing[c].at[pl.ds((dx - 1) * ny, ny)],
            dst_ref=piece(received, origin * ny, ny, c),
            send_sem=g_send.at[c, dx - 1],
            recv_sem=g_recv.at[c, dx - 1],
            device_id=(peer, gy, gz),
            device_id_type=MESH,
        )

    def either(c, code):
        held = pool[c][jnp.minimum(code, slots + near - 1)]
        came = inflow[c][jnp.clip(code - slots - near, 0, far - 1)]
        return jnp.where(code < slots + near, held, came)

    def send_inward(c, crosses, relays):
        load(c).wait()
        for dz in range(1, depth):
            origin = lax.rem(gz + depth - dz, depth)
            y_copy(c, dz, origin, origin).wait_recv()
        if relays:
            near_copy(c, outer).wait_recv()

        @pl.loop(0, far if crosses else near)
        def _(p):
            inward[c][p] = pool[c][plan[0, at["inward"] + p]]

        if crosses:
            cross_copy(c, inner).start()
        else:
            near_copy(c, inner).start()

    def deliver(c, crosses, relays):
        if crosses:
            cross_copy(c, inner).wait_recv()
        else:
            back_copy(c, inner).wait_recv()
        if relays:

            @pl.loop(0, back)
            def _(p):
                outward[c][p] = either(c, plan[0, at["outward"] + p])

            back_copy(c, outer).start()

        @pl.loop(0, (nx - 1) * ny)
        def _(k):
            outgoing[c][k] = either(c, plan[0, at["deliver"] + ny + k])

        for dx in range(1, nx):
            g_copy(c, dx, lax.rem(gx + dx, nx), gx).start()

        @pl.loop(0, ny)
        def _(k):
            row, rows, column, columns = pieces[c]
            received[gx * ny + k, pl.ds(row, rows), pl.ds(column, columns)] = either(
                c, plan[0, at["deliver"] + k]
            )

    def stream(crosses, relays):
        area = [rows * columns / (pieces[-1][0] + pieces[-1][1]) for _, rows, _, columns in pieces]
        area = [a * 16 / sum(area) for a in area]
        events = []
        for c in range(chunks):
            upto = sum(area[: c + 1])
            sent = near * (upto - area[c])
            landed = near * area[0] + far * (upto + area[c]) + LATENCY
            if crosses or relays:
                sent, landed = c, c + AHEAD + 0.5
            events.append((sent, 0, c))
            events.append((landed, 1, c))
        for _, kind, c in sorted(events):
            if kind == 0:
                send_inward(c, crosses, relays)
            else:
                deliver(c, crosses, relays)
        for c in range(chunks):
            if crosses:
                cross_copy(c, inner).wait_send()
            else:
                near_copy(c, inner).wait_send()
            if relays:
                back_copy(c, outer).wait_send()

    fetch = pltpu.make_async_copy(plan_ref, plan, plan_sem)
    fetch.start()
    for c in range(chunks):
        load(c).start()
    barrier = pltpu.get_barrier_semaphore()
    for dz in range(1, depth):
        pl.semaphore_signal(
            barrier, inc=1, device_id=(gx, gy, lax.rem(gz + dz, depth)), device_id_type=MESH
        )
    for dx in range(1, nx):
        pl.semaphore_signal(
            barrier, inc=1, device_id=(lax.rem(gx + dx, nx), gy, gz), device_id_type=MESH
        )
    pl.semaphore_signal(barrier, inc=1, device_id=(gx, inner, gz), device_id_type=MESH)

    @pl.when(level > 0)
    def _():
        pl.semaphore_signal(barrier, inc=1, device_id=(gx, outer, gz), device_id_type=MESH)

    pl.semaphore_wait(barrier, depth - 1 + nx - 1 + 1 + jnp.where(level > 0, 1, 0))
    for c in range(chunks):
        for dz in range(1, depth):
            y_copy(c, dz, lax.rem(gz + dz, depth), gz).start()
    fetch.wait()

    if half == 1:
        stream(True, False)
    else:
        pl.when(level == 0)(lambda: stream(False, False))
        pl.when(middle)(lambda: stream(True, True))
        if half > 2:
            pl.when((level > 0) & jnp.logical_not(middle))(lambda: stream(False, True))

    for c in range(chunks):
        for dz in range(1, depth):
            y_copy(c, dz, lax.rem(gz + dz, depth), gz).wait_send()
        for dx in range(1, nx):
            origin = lax.rem(gx + nx - dx, nx)
            g_copy(c, dx, origin, origin).wait()


def count(mask):
    return jnp.sum(mask.astype(jnp.int32), axis=1)


def pick(value, mask, position, wanted):
    hit = mask[None, :] & (position[None, :] == jnp.arange(wanted, dtype=jnp.int32)[:, None])
    return jnp.sum(jnp.where(hit, value[None, :], 0), axis=1)


def shards(embeds, dest_device, shuffle_key, lengths, gain):
    tiles_here, tile_rows, width = embeds.shape
    nx, ny, depth = lax.axis_size("gx"), lax.axis_size("gy"), lax.axis_size("gz")
    devices = nx * ny * depth
    per_peer = (tiles_here + depth - 1) // depth
    slots = depth * per_peer
    half = ny // 2
    cap = 2 * tiles_here
    if ny % 2 or tile_rows % 128 or width % 512 or slots > tiles_here:
        return direct(embeds, dest_device, shuffle_key, lengths, gain)

    most = half * min(tiles_here, nx * half)
    near_most = max([(e + 1) * min(tiles_here, nx * (ny - 1 - e)) for e in range(half - 1)] + [1])
    back_most = max([(ny - e) * min(tiles_here, nx * e) for e in range(1, half)] + [1])
    classes = sorted({max(near_most, most * part // 16) for part in CLASSES})

    vmem = pl.BlockSpec(memory_space=pltpu.VMEM)
    smem = pl.BlockSpec(memory_space=pltpu.SMEM)
    hbm = pl.BlockSpec(memory_space=pl.ANY)
    lanes = -(-tiles_here // 128) * 128
    table, normed = pl.pallas_call(
        functools.partial(table_kernel, (nx, ny, depth, per_peer)),
        out_shape=(
            jax.ShapeDtypeStruct((devices, 2, lanes), jnp.int32),
            pltpu.HBM((slots, tile_rows, width), jnp.bfloat16),
        ),
        in_specs=[pl.BlockSpec(memory_space=pltpu.HBM)] * 5,
        out_specs=(vmem, pl.BlockSpec(memory_space=pltpu.HBM)),
        scratch_shapes=[
            pltpu.SMEM((1, tiles_here), jnp.int32),
            pltpu.SMEM((1, lengths.shape[0]), jnp.int32),
            pltpu.VMEM((1, tiles_here), jnp.int32),
            pltpu.VMEM((1, tiles_here), jnp.int32),
            pltpu.VMEM((1, width), jnp.float32),
            pltpu.SemaphoreType.DMA((5,)),
            pltpu.VMEM((2, lanes), jnp.int32),
            pltpu.SMEM((slots,), jnp.int32),
            pltpu.SMEM((slots,), jnp.int32),
            pltpu.VMEM((tiles_here, tile_rows, width), jnp.bfloat16),
            pltpu.VMEM((slots, tile_rows, width), jnp.bfloat16),
            pltpu.SemaphoreType.DMA((devices - 1,)),
            pltpu.SemaphoreType.DMA((devices - 1,)),
            pltpu.SemaphoreType.DMA,
            pltpu.SemaphoreType.DMA((slots,)),
        ],
        compiler_params=pltpu.CompilerParams(
            collective_id=0, has_side_effects=True, vmem_limit_bytes=56 * 1024 * 1024
        ),
        name="tables",
    )(dest_device[None, :], shuffle_key[None, :], lengths[None, :], embeds, gain.reshape(1, width))

    gx, gy, gz = lax.axis_index("gx"), lax.axis_index("gy"), lax.axis_index("gz")
    group = gx * ny + gy
    me = group * depth + gz
    dest = table[:, 0, :tiles_here].reshape(-1)
    keys = table[:, 1, :tiles_here].reshape(-1)
    order = jnp.arange(devices * tiles_here, dtype=jnp.int32)
    before = order[None, :] < order[:, None]
    source = order // tiles_here
    from_x, from_y = source // (ny * depth), source // depth % ny
    to_x, to_y, to_z = dest // (ny * depth), dest // depth % ny, dest % depth

    bounds = jnp.arange(ny - 1, dtype=jnp.int32)
    lane = from_x * depth + to_z
    hop_up = (from_y[None, :] <= bounds[:, None]) & (to_y[None, :] > bounds[:, None])
    hop_down = (from_y[None, :] > bounds[:, None]) & (to_y[None, :] <= bounds[:, None])
    hops = jnp.concatenate([hop_up, hop_down])
    in_lane = lane[None, :] == jnp.arange(nx * depth, dtype=jnp.int32)[:, None]
    load = jnp.sum((hops[:, None, :] & in_lane[None, :, :]).astype(jnp.int32), axis=2)

    low = gy < half
    level = jnp.where(low, gy, ny - 1 - gy)
    depth_from = jnp.where(low, from_y, ny - 1 - from_y)
    depth_to = jnp.where(low, to_y, ny - 1 - to_y)
    in_my_lane = (from_x == gx) & (to_z == gz)
    inward = in_my_lane & (depth_from <= level) & (depth_to > level)
    near_in = in_my_lane & (depth_from < level) & (depth_to >= level)
    outward = in_my_lane & (depth_from >= level) & (depth_to < level)
    far_in = in_my_lane & (depth_from > level) & (depth_to <= level)
    landing = in_my_lane & (depth_to == level)
    to_me = dest == me

    same_source = source[:, None] == source[None, :]
    spot = count(before & same_source & (to_z[:, None] == to_z[None, :]))
    at_inward = count(before & inward[None, :])
    at_near = count(before & near_in[None, :])
    at_outward = count(before & outward[None, :])
    at_far = count(before & far_in[None, :])
    at_landing = count(before & (landing[None, :] & (to_x[:, None] == to_x[None, :])))
    at_me = count(before & (to_me[None, :] & (from_x[:, None] == from_x[None, :])))
    rank = count((keys[None, :] < keys[:, None]) & to_me[None, :])
    own_slot = source % depth * per_peer + spot

    over = load.reshape(-1)[None, :] > jnp.array(classes[:-1], jnp.int32)[:, None]
    chosen = jnp.sum(jnp.any(over, axis=1).astype(jnp.int32))
    code = jnp.where(
        depth_from == level,
        own_slot,
        jnp.where(depth_from < level, slots + at_near, slots + near_most + at_far),
    )
    parts = {
        "inward": pick(code, inward, at_inward, most),
        "outward": pick(code, outward, at_outward, back_most),
        "deliver": pick(code, landing, (to_x - gx) % nx * ny + at_landing, nx * ny),
    }
    at, total = {}, 0
    for name, part in parts.items():
        at[name] = total
        total += part.shape[0]
    plan = jnp.pad(jnp.concatenate(list(parts.values())), (0, -total % 128))[None, :]
    which = pick(from_x * ny + at_me + 1, to_me, rank, cap)

    pieces, done = [], 0
    for part in CHUNKS:
        row, column = done // 4 * tile_rows // 16, done % 4 * width // 4
        if part % 4 == 0:
            pieces.append((row, part // 4 * tile_rows // 16, 0, width))
        else:
            pieces.append((row, tile_rows // 16, column, part * width // 4))
        done += part
    pieces = tuple(pieces)
    chunks = len(pieces)

    def branch(index, far):
        def run(plan, normed, chosen_rows, filled):
            near, back = near_most, min(far, back_most)
            counts = ((slots + near,), (far,), (far,), (back,), ((nx - 1) * ny,))
            received = pl.pallas_call(
                functools.partial(
                    line_kernel, (nx, ny, depth, per_peer, pieces, near, far, back, at)
                ),
                out_shape=pltpu.VMEM((nx * ny, tile_rows, width), jnp.bfloat16),
                in_specs=[hbm, pl.BlockSpec(memory_space=pltpu.HBM)],
                out_specs=vmem,
                scratch_shapes=[
                    pltpu.SMEM(plan.shape, jnp.int32),
                    pltpu.SemaphoreType.DMA,
                    pltpu.SemaphoreType.DMA((chunks,)),
                    pltpu.SemaphoreType.DMA((chunks, depth - 1)),
                    pltpu.SemaphoreType.DMA((chunks, depth - 1)),
                    pltpu.SemaphoreType.DMA((chunks,)),
                    pltpu.SemaphoreType.DMA((chunks,)),
                    pltpu.SemaphoreType.DMA((chunks,)),
                    pltpu.SemaphoreType.DMA((chunks,)),
                    pltpu.SemaphoreType.DMA((chunks, nx - 1)),
                    pltpu.SemaphoreType.DMA((chunks, nx - 1)),
                ]
                + [
                    pltpu.VMEM((*lead, rows, columns), jnp.bfloat16)
                    for lead in counts
                    for _, rows, _, columns in pieces
                ],
                compiler_params=pltpu.CompilerParams(
                    collective_id=1 + index, has_side_effects=True, vmem_limit_bytes=44 * 1024 * 1024
                ),
                name=f"line{far}",
            )(plan, normed)
            return pl.pallas_call(
                place_kernel,
                out_shape=pltpu.HBM((cap, tile_rows, width), jnp.bfloat16),
                in_specs=[smem, smem, vmem],
                out_specs=pl.BlockSpec(memory_space=pltpu.HBM),
                scratch_shapes=[
                    pltpu.VMEM((tile_rows, width), jnp.bfloat16),
                    pltpu.SemaphoreType.DMA((cap,)),
                ],
                compiler_params=pltpu.CompilerParams(vmem_limit_bytes=24 * 1024 * 1024),
                name="place",
            )(chosen_rows, filled, received)

        return run

    return lax.switch(
        chosen,
        [branch(i, far) for i, far in enumerate(classes)],
        plan,
        normed,
        jnp.maximum(which - 1, 0),
        (which > 0).astype(jnp.int32),
    )


def solution(mesh):
    return jax.shard_map(
        shards,
        mesh=mesh,
        in_specs=(
            P(("gx", "gy", "gz"), None, None),
            P(("gx", "gy", "gz")),
            P(("gx", "gy", "gz")),
            P(),
            P(),
        ),
        out_specs=P(("gx", "gy", "gz"), None, None),
        check_vma=False,
    )
```

profile of v0, /device:TPU:1, one launch (start us, length us, event | category | flops | bytes accessed | tf_op | source)
XLA Modules:
  0.0 169.4 jit_solution(9069518923359141116)
XLA Ops:
  0.0 12.0 %tables.1 = (s32[32,2,128]{2,1,0:T(2,128)}, bf16[8,128,2048]{2,1,0:T(8,128)(2,1)}) custom-call(s32[1,8]{1,0:T(1,128)} %bitcast.17, s32[1,8]{1,0:T(1,128)} %bitcast.18, s32[1,8]{1,0:T(1,128)} %bitcast.19, bf16[8,128,2048]{2,1,0:T(8,128)(2,1)} %x_ref.1, f32[1,2048]{1,0:T(1,128)} %bitcast.16), custom_call_target="tpu_custom_call" | custom-call | tf_op jit(solution)/shard_map/tables/pallas_call | solution.py:652
  12.1 0.9 slice_reduce_fusion
  13.0 0.1 lt.127
  13.1 0.1 reshape_squeeze.3
  13.2 0.2 convert_reduce_fusion.6
  13.5 0.3 convert_reduce_fusion.1
  13.8 0.1 select_reduce_fusion
  13.9 0.2 convert_reduce_fusion.8
  14.1 0.1 gt.57
  14.2 0.8 compare_reduce_fusion
  15.0 0.6 convert_reduce_fusion.9
  16.4 0.2 convert_reduce_fusion.2
  16.6 0.2 convert_reduce_fusion.5
  16.8 0.1 select_reduce_fusion.3
  16.9 0.1 select_reduce_fusion.2
  17.0 0.1 pad_add_fusion.1
  17.1 152.1 %conditional.1 = (bf16[16,128,2048]{2,1,0:T(8,128)(2,1)}) conditional(s32[]{:T(128)} %clamp.3, (s32[44]{0:T(128)S(1)}, bf16[8,128,2048]{2,1,0:T(8,128)(2,1)}, s32[16]{0:T(128)S(1)}, s32[16]{0:T(128)S(1)}, s32[16]{0:T(128)S(1)}, /*index=5*/s32[]{:T(128)}, s32[]{:T(128)}) %tuple.23, (s32[44]{0:T(128)S(1)}, ...), branch_computations={%region_15.16_spmd, %region_16.17_spmd, %region_17.18_spmd, %regio... | conditional | flops 32 | bytes 896 | solution.py:804
  17.3 147.3 %line11.1.blocks_ref = bf16[16,128,2048]{2,1,0:T(8,128)(2,1)S(1)} custom-call(s32[1,128]{1,0:T(1,128)S(1)} %pad_bitcast_fusion.2.plan_ref, bf16[8,128,2048]{2,1,0:T(8,128)(2,1)} %get-tuple-element.71.x_ref), custom_call_target="tpu_custom_call" | custom-call | tf_op jit(solution)/shard_map/cond/branch_2_fun/line11/pallas_call | solution.py:759
  164.6 4.0 %place.8 = bf16[16,128,2048]{2,1,0:T(8,128)(2,1)} custom-call(s32[16]{0:T(128)S(1)} %add_maximum_fusion.2.source_ref, s32[16]{0:T(128)S(1)} %get-tuple-element.69.filled_ref, bf16[16,128,2048]{2,1,0:T(8,128)(2,1)S(1)} %line11.1.blocks_ref), custom_call_target="tpu_custom_call" | custom-call | tf_op jit(solution)/shard_map/cond/branch_2_fun/place/pallas_call | solution.py:789
  (17 shorter events, 0.2 us)
where the time goes:
time: 170 us; the launch traced here: 169 us
  Pallas kernels  163 us (96%)
  other arithmetic  3.16 us (2%)
    pallas_call x1, Pallas kernels, run(): pl.pallas_call(functools.partial(line_kernel, (nx, ny, depth, per_peer, p...  147 us
    pallas_call x1, Pallas kernels, shards(): pl.pallas_call(functools.partial(table_kernel, (nx, ny, depth, per_peer))...  12 us
    pallas_call x1, Pallas kernels, run(): pl.pallas_call(place_kernel, out_shape=pltpu.HBM((cap, tile_rows, width),...  3.96 us

commit v1 on v0

--- a/solution.py
+++ b/solution.py
@@ -337,8 +337,8 @@
 
 
 def table_kernel(
-    sizes, dest_hbm, key_hbm, lengths_hbm, x_ref, gain_hbm, table_ref, normed_ref,
-    dest_ref, lengths_ref, dest_row, key_row, gain_ref, small_sem, mine, first_table, limit_table, raw, done, send, recv, x_sem, out_sem,
+    sizes, dest_hbm, key_hbm, lengths_hbm, x_ref, gain_hbm, table_ref, normed_ref, early_ref,
+    dest_ref, lengths_ref, dest_row, key_row, gain_ref, small_sem, mine, first_table, limit_table, raw, done, send, recv, x_sem, out_sem, y_send, y_recv,
 ):
     nx, ny, depth, per_peer = sizes
     devices = nx * ny * depth
@@ -360,17 +360,34 @@
             device_id_type=MESH,
         )
 
-    def normalize(slot):
-        @pl.loop(0, tile_rows // block, unroll=4)
-        def _(part):
-            start = part * block
+    gx, gy, gz = lax.axis_index("gx"), lax.axis_index("gy"), lax.axis_index("gz")
+
+    def early_copy(dz, peer, origin):
+        return pltpu.make_async_remote_copy(
+            src_ref=done.at[pl.ds(peer * per_peer, per_peer), pl.ds(0, early_ref.shape[1])],
+            dst_ref=early_ref.at[pl.ds(origin * per_peer, per_peer)],
+            send_sem=y_send.at[dz - 1],
+            recv_sem=y_recv.at[dz - 1],
+            device_id=(gx, gy, peer),
+            device_id_type=MESH,
+        )
+
+    def store(part):
+        rows = pl.ds(part * block, block)
+        return pltpu.make_async_copy(done.at[:, rows], normed_ref.at[:, rows], out_sem.at[part])
+
+    def normalize(part):
+        start = part * block
+
+        @pl.loop(0, slots, unroll=4)
+        def _(slot):
             values = raw[first_table[slot], pl.ds(start, block)].astype(jnp.float32)
             meansq = jnp.mean(values * values, axis=-1, keepdims=True)
             scaled = values * lax.rsqrt(jnp.maximum(meansq, 0.25)) * gain_ref[...]
             row = start + lax.broadcasted_iota(jnp.int32, (block, 1), 0)
             done[slot, pl.ds(start, block)] = jnp.where(row < limit_table[slot], scaled, 0.0).astype(jnp.bfloat16)
 
-        pltpu.make_async_copy(done.at[slot], normed_ref.at[slot], out_sem.at[slot]).start()
+        store(part).start()
 
     small = [
         pltpu.make_async_copy(dest_hbm, dest_row, small_sem.at[0]),
@@ -416,18 +433,24 @@
         limit_table[slot] = limit
 
     load.wait()
-    for slot in range(slots):
-        normalize(slot)
+    for part in range(tile_rows // block):
+        normalize(part)
+        if part == 0:
+            for dz in range(1, depth):
+                early_copy(dz, lax.rem(gz + dz, depth), gz).start()
     for step in range(1, devices):
         source = lax.rem(me + devices - step, devices)
         row_copy(step, source, source).wait()
-    for slot in range(slots):
-        pltpu.make_async_copy(done.at[slot], normed_ref.at[slot], out_sem.at[slot]).wait()
+    for dz in range(1, depth):
+        origin = lax.rem(gz + depth - dz, depth)
+        early_copy(dz, origin, origin).wait()
+    for part in range(tile_rows // block):
+        store(part).wait()
 
 
 def line_kernel(
-    sizes, plan_ref, x_ref, received,
-    plan, plan_sem, x_sem, y_send, y_recv, a_send, a_recv, b_send, b_recv,
+    sizes, plan_ref, x_ref, early_ref, received,
+    plan, plan_sem, x_sem, early_sem, y_send, y_recv, a_send, a_recv, b_send, b_recv,
     g_send, g_recv, *buffers,
 ):
     nx, ny, depth, per_peer, pieces, near, far, back, at = sizes
@@ -455,6 +478,16 @@
             x_sem.at[c],
         )
 
+    ready = [c for c in range(chunks) if pieces[c][0] + pieces[c][1] <= early_ref.shape[1]]
+
+    def early_load(c, dz):
+        origin = lax.rem(gz + depth - dz, depth)
+        return pltpu.make_async_copy(
+            piece(early_ref, origin * per_peer, per_peer, c),
+            pool[c].at[pl.ds(origin * per_peer, per_peer)],
+            early_sem.at[c, dz - 1],
+        )
+
     def y_copy(c, dz, peer, origin):
         return pltpu.make_async_remote_copy(
             src_ref=piece(x_ref, peer * per_peer, per_peer, c),
@@ -514,7 +547,10 @@
         load(c).wait()
         for dz in range(1, depth):
             origin = lax.rem(gz + depth - dz, depth)
-            y_copy(c, dz, origin, origin).wait_recv()
+            if c in ready:
+                early_load(c, dz).wait()
+            else:
+                y_copy(c, dz, origin, origin).wait_recv()
         if relays:
             near_copy(c, outer).wait_recv()
 
@@ -583,6 +619,9 @@
     fetch.start()
     for c in range(chunks):
         load(c).start()
+        if c in ready:
+            for dz in range(1, depth):
+                early_load(c, dz).start()
     barrier = pltpu.get_barrier_semaphore()
     for dz in range(1, depth):
         pl.semaphore_signal(
@@ -599,7 +638,7 @@
         pl.semaphore_signal(barrier, inc=1, device_id=(gx, outer, gz), device_id_type=MESH)
 
     pl.semaphore_wait(barrier, depth - 1 + nx - 1 + 1 + jnp.where(level > 0, 1, 0))
-    for c in range(chunks):
+    for c in range(len(ready), chunks):
         for dz in range(1, depth):
             y_copy(c, dz, lax.rem(gz + dz, depth), gz).start()
     fetch.wait()
@@ -613,8 +652,9 @@
             pl.when((level > 0) & jnp.logical_not(middle))(lambda: stream(False, True))
 
     for c in range(chunks):
-        for dz in range(1, depth):
-            y_copy(c, dz, lax.rem(gz + dz, depth), gz).wait_send()
+        if c not in ready:
+            for dz in range(1, depth):
+                y_copy(c, dz, lax.rem(gz + dz, depth), gz).wait_send()
         for dx in range(1, nx):
             origin = lax.rem(gx + nx - dx, nx)
             g_copy(c, dx, origin, origin).wait()
@@ -649,14 +689,16 @@
     smem = pl.BlockSpec(memory_space=pltpu.SMEM)
     hbm = pl.BlockSpec(memory_space=pl.ANY)
     lanes = -(-tiles_here // 128) * 128
-    table, normed = pl.pallas_call(
+    early_rows = tile_rows // 16
+    table, normed, early = pl.pallas_call(
         functools.partial(table_kernel, (nx, ny, depth, per_peer)),
         out_shape=(
             jax.ShapeDtypeStruct((devices, 2, lanes), jnp.int32),
             pltpu.HBM((slots, tile_rows, width), jnp.bfloat16),
+            pltpu.HBM((slots, early_rows, width), jnp.bfloat16),
         ),
         in_specs=[pl.BlockSpec(memory_space=pltpu.HBM)] * 5,
-        out_specs=(vmem, pl.BlockSpec(memory_space=pltpu.HBM)),
+        out_specs=(vmem, pl.BlockSpec(memory_space=pltpu.HBM), pl.BlockSpec(memory_space=pltpu.HBM)),
         scratch_shapes=[
             pltpu.SMEM((1, tiles_here), jnp.int32),
             pltpu.SMEM((1, lengths.shape[0]), jnp.int32),
@@ -672,7 +714,9 @@
             pltpu.SemaphoreType.DMA((devices - 1,)),
             pltpu.SemaphoreType.DMA((devices - 1,)),
             pltpu.SemaphoreType.DMA,
-            pltpu.SemaphoreType.DMA((slots,)),
+            pltpu.SemaphoreType.DMA((tile_rows // 16,)),
+            pltpu.SemaphoreType.DMA((depth - 1,)),
+            pltpu.SemaphoreType.DMA((depth - 1,)),
         ],
         compiler_params=pltpu.CompilerParams(
             collective_id=0, has_side_effects=True, vmem_limit_bytes=56 * 1024 * 1024
@@ -753,7 +797,7 @@
     chunks = len(pieces)
 
     def branch(index, far):
-        def run(plan, normed, chosen_rows, filled):
+        def run(plan, normed, early, chosen_rows, filled):
             near, back = near_most, min(far, back_most)
             counts = ((slots + near,), (far,), (far,), (back,), ((nx - 1) * ny,))
             received = pl.pallas_call(
@@ -761,12 +805,13 @@
                     line_kernel, (nx, ny, depth, per_peer, pieces, near, far, back, at)
                 ),
                 out_shape=pltpu.VMEM((nx * ny, tile_rows, width), jnp.bfloat16),
-                in_specs=[hbm, pl.BlockSpec(memory_space=pltpu.HBM)],
+                in_specs=[hbm] + [pl.BlockSpec(memory_space=pltpu.HBM)] * 2,
                 out_specs=vmem,
                 scratch_shapes=[
                     pltpu.SMEM(plan.shape, jnp.int32),
                     pltpu.SemaphoreType.DMA,
                     pltpu.SemaphoreType.DMA((chunks,)),
+                    pltpu.SemaphoreType.DMA((chunks, depth - 1)),
                     pltpu.SemaphoreType.DMA((chunks, depth - 1)),
                     pltpu.SemaphoreType.DMA((chunks, depth - 1)),
                     pltpu.SemaphoreType.DMA((chunks,)),
@@ -785,7 +830,7 @@
                     collective_id=1 + index, has_side_effects=True, vmem_limit_bytes=44 * 1024 * 1024
                 ),
                 name=f"line{far}",
-            )(plan, normed)
+            )(plan, normed, early)
             return pl.pallas_call(
                 place_kernel,
                 out_shape=pltpu.HBM((cap, tile_rows, width), jnp.bfloat16),
@@ -806,6 +851,7 @@
         [branch(i, far) for i, far in enumerate(classes)],
         plan,
         normed,
+        early,
         jnp.maximum(which - 1, 0),
         (which > 0).astype(jnp.int32),
     )

time: 170 us -> 157 us (0.924)
  Pallas kernels: 163 us -> 151 us
    pallas_call x1, Pallas kernels: 147 us -> 134 us  [run(): pl.pallas_call(functools.partial(line_kernel, (nx, ny, depth, per_peer, p...]
where the time goes in v1:
time: 157 us
  Pallas kernels  151 us (96%)
  other arithmetic  3.16 us (2%)
    pallas_call x1, Pallas kernels, run(): pl.pallas_call(functools.partial(line_kernel, (nx, ny, depth, per_peer, p...  134 us
    pallas_call x1, Pallas kernels, shards(): pl.pallas_call(functools.partial(table_kernel, (nx, ny, depth, per_peer))...  13 us
    pallas_call x1, Pallas kernels, run(): pl.pallas_call(place_kernel, out_shape=pltpu.HBM((cap, tile_rows, width),...  3.96 us

profile of v1, /device:TPU:1, one launch (start us, length us, event | category | flops | bytes accessed | tf_op | source)
XLA Modules:
  0.0 157.0 jit_solution(4624184758313202425)
XLA Ops:
  0.0 13.0 %tables.1 = (s32[32,2,128]{2,1,0:T(2,128)}, bf16[8,128,2048]{2,1,0:T(8,128)(2,1)}, bf16[8,8,2048]{2,1,0:T(8,128)(2,1)}) custom-call(s32[1,8]{1,0:T(1,128)} %bitcast.17, s32[1,8]{1,0:T(1,128)} %bitcast.18, s32[1,8]{1,0:T(1,128)} %bitcast.19, bf16[8,128,2048]{2,1,0:T(8,128)(2,1)} %x_ref.1, f32[1,2048]{1,0:T(1,128)} %bitcast.16), custom_call_target="tpu_custom_call" | custom-call | tf_op jit(solution)/shard_map/tables/pallas_call | solution.py:693
  13.1 0.9 slice_reduce_fusion
  14.0 0.1 lt.127
  14.1 0.1 reshape_squeeze.3
  14.2 0.2 convert_reduce_fusion.6
  14.5 0.3 convert_reduce_fusion.1
  14.8 0.1 select_reduce_fusion
  14.9 0.2 convert_reduce_fusion.8
  15.1 0.1 gt.57
  15.2 0.8 compare_reduce_fusion
  16.0 0.6 convert_reduce_fusion.9
  17.4 0.2 convert_reduce_fusion.2
  17.6 0.2 convert_reduce_fusion.5
  17.8 0.1 select_reduce_fusion.3
  17.9 0.1 select_reduce_fusion.2
  18.0 0.1 pad_add_fusion.1
  18.1 138.6 %conditional.1 = (bf16[16,128,2048]{2,1,0:T(8,128)(2,1)}) conditional(s32[]{:T(128)} %clamp.3, (s32[44]{0:T(128)S(1)}, bf16[8,128,2048]{2,1,0:T(8,128)(2,1)}, bf16[8,8,2048]{2,1,0:T(8,128)(2,1)}, s32[16]{0:T(128)S(1)}, s32[16]{0:T(128)S(1)}, /*index=5*/s32[16]{0:T(128)S(1)}, s32[]{:T(128)}, s32[]{:T(128)}) %tuple.23, ...), branch_computations={%region_15.16_spmd, %region_16.17_spmd, %region_17.18_spmd, %regio... | conditional | flops 32 | bytes 896 | solution.py:849
  18.1 133.8 %line10.1.blocks_ref = bf16[16,128,2048]{2,1,0:T(8,128)(2,1)S(1)} custom-call(s32[1,128]{1,0:T(1,128)S(1)} %pad_bitcast_fusion.1.plan_ref, bf16[8,128,2048]{2,1,0:T(8,128)(2,1)} %get-tuple-element.80.x_ref, bf16[8,8,2048]{2,1,0:T(8,128)(2,1)} %get-tuple-element.81.early_ref), custom_call_target="tpu_custom_call" | custom-call | tf_op jit(solution)/shard_map/cond/branch_1_fun/line10/pallas_call | solution.py:803
  151.9 4.0 %place.7 = bf16[16,128,2048]{2,1,0:T(8,128)(2,1)} custom-call(s32[16]{0:T(128)S(1)} %add_maximum_fusion.1.source_ref, s32[16]{0:T(128)S(1)} %get-tuple-element.78.filled_ref, bf16[16,128,2048]{2,1,0:T(8,128)(2,1)S(1)} %line10.1.blocks_ref), custom_call_target="tpu_custom_call" | custom-call | tf_op jit(solution)/shard_map/cond/branch_1_fun/place/pallas_call | solution.py:834
  (17 shorter events, 0.2 us)
